TPU v7x, 32 devices: a whole 2x2x4 slice. The times are simulated.
32 devices in a mesh: row: 8 (over z, y), col: 4 (over x, core).
Axes of the slice: x: 2, y: 2, z: 4, core: 2. Of those that a mesh axis runs over, the one named last changes fastest.
Arguments:
- prior: float32 [2, 4096, 4096], P(None, 'row', 'col'), may hold values from 0.1 to 10
- first_tiles: bfloat16 [2, 32, 24, 128, 128], P(None, 'row'), may hold values from 0 to 1
- first_columns: int32 [2, 32, 24], P(None, 'row'), may hold values from 0 to 31, as said below
- first_counts: int32 [2, 32], P(None, 'row'), may hold values from 1 to 24, as said below
- second_network_tiles: bfloat16 [2, 32, 24, 128, 128], P(None, 'col'), may hold values from 0 to 1
- second_columns: int32 [2, 32, 24], P(None, 'col'), may hold values from 0 to 31, as said below
- second_counts: int32 [2, 32], P(None, 'col'), may hold values from 1 to 24, as said below
- sizes_first: int32 [2], replicated, may hold values from 2048 to 4096
- sizes_second: int32 [2], replicated, may hold values from 2048 to 4096
Outputs:
- similarity: float32 [2, 4096, 4096], P(None, 'row', 'col')
Inputs may be any that keep to these rules, and one draw needn't show every extreme that they name: `first_columns`: within a tile row the 24 slots name distinct tile columns. Only the first first_counts[p, i] slots of tile row i are live; in every pair some tile row has all 24 live. `second_columns`: within a tile row the 24 slots name distinct tile columns. Only the first second_counts[p, i] slots of tile row i are live; in every pair some tile row has all 24 live.
All inputs are finite; a program needn't handle non-finite values.
Results may differ from a plain program's by a relative error of at most 0.00035.
Values may be sent and summed in bfloat16 or wider, within the bound.
A program may use at most 128 MiB of HBM per device.

v0:
```python
import jax
import jax.numpy as jnp
from jax import lax
from jax.sharding import PartitionSpec as P

ITERS = 2
propagation = 0.7


def first_local(tiles, columns, counts, panel):
    local_rows = tiles.shape[0]
    tile_size = tiles.shape[2]
    width = panel.shape[1]
    blocks = panel.reshape(-1, tile_size, width)
    selected_entries = blocks[columns]
    in_use = jnp.arange(tiles.shape[1])[None, :] < counts[:, None]
    masked_entries = jnp.where(in_use[:, :, None, None], tiles, jnp.zeros((), tiles.dtype))
    similarity_output = jnp.einsum(
        "hgfu,hguq->hfq", masked_entries, selected_entries, preferred_element_type=jnp.float32
    )
    return similarity_output.reshape(local_rows * tile_size, width)


def second_local(tiles, columns, counts, gathered):
    local_rows = tiles.shape[0]
    tile_size = tiles.shape[2]
    height = gathered.shape[0]
    blocks = gathered.reshape(height, -1, tile_size)
    selected_entries = blocks[:, columns]
    in_use = jnp.arange(tiles.shape[1])[None, :] < counts[:, None]
    masked_entries = jnp.where(in_use[:, :, None, None], tiles, jnp.zeros((), tiles.dtype))
    similarity_output = jnp.einsum(
        "rtsk,tsck->rtc", selected_entries, masked_entries, preferred_element_type=jnp.float32
    )
    return similarity_output.reshape(height, local_rows * tile_size)


def advance(
    current,
    initial,
    active,
    entries,
    first_network_tiles,
    f_columns,
    f_counts,
    s_tiles,
    s_columns,
    s_counts,
):
    resident_panel_block = current.astype(jnp.bfloat16)
    panel = lax.all_gather(resident_panel_block, "row", axis=1, tiled=True)
    product = jnp.stack([first_local(first_network_tiles[0], f_columns[0], f_counts[0], panel[0])])
    product = product.astype(jnp.bfloat16)
    gathered = lax.all_gather(product, "col", axis=2, tiled=True)
    image = jnp.stack([second_local(s_tiles[0], s_columns[0], s_counts[0], gathered[0])])
    image = jnp.where(active, image, jnp.float32(0.0))
    square_sum = lax.psum(jnp.sum(image * image, axis=(1, 2)), ("row", "col"))
    divisor = jnp.sqrt(square_sum / entries + 1e-06)
    return propagation * image / divisor[:, None, None] + (1.0 - propagation) * initial


def shards(
    prior,
    first_tiles,
    first_columns,
    first_counts,
    second_network_tiles,
    second_columns,
    second_counts,
    sizes_first,
    sizes_second,
):
    pair_count, row_count, col_count = prior.shape
    row_index = lax.axis_index("row") * row_count + jnp.arange(row_count, dtype=jnp.int32)
    col_index = lax.axis_index("col") * col_count + jnp.arange(col_count, dtype=jnp.int32)
    active = (row_index[None, :, None] < sizes_first[:, None, None]) & (
        col_index[None, None, :] < sizes_second[:, None, None]
    )
    initial = jnp.where(active, prior, jnp.float32(0.0))
    entries = sizes_first.astype(jnp.float32) * sizes_second.astype(jnp.float32)
    current = initial
    for iteration in range(ITERS):
        updated = []
        for pair_index in range(pair_count):
            upper = pair_index + 1
            updated.append(
                advance(
                    current[pair_index:upper],
                    initial[pair_index:upper],
                    active[pair_index:upper],
                    entries[pair_index:upper],
                    first_tiles[pair_index:upper],
                    first_columns[pair_index:upper],
                    first_counts[pair_index:upper],
                    second_network_tiles[pair_index:upper],
                    second_columns[pair_index:upper],
                    second_counts[pair_index:upper],
                )
            )
        current = jnp.concatenate(updated, axis=0)
    return current


def solution(mesh):
    in_specs = (
        P(None, "row", "col"),
        P(None, "row", None, None, None),
        P(None, "row", None),
        P(None, "row"),
        P(None, "col", None, None, None),
        P(None, "col", None),
        P(None, "col"),
        P(),
        P(),
    )
    out_specs = P(None, "row", "col")
    return jax.shard_map(shards, mesh=mesh, in_specs=in_specs, out_specs=out_specs, check_vma=False)
```

profile of v0, /device:TPU:0, one launch (start us, length us, event | category | flops | bytes accessed | tf_op | source)
XLA Modules:
  0.0 844.6 jit_solution(2062341585849978496)
XLA Ops:
  6.5 0.7 broadcast_compare_fusion
  7.3 0.7 broadcast_compare_fusion.1
  8.0 2.7 broadcast_select_fusion
  10.7 2.0 copy-done
  12.7 1.7 fusion.24
  14.5 0.7 all-gather.9.cloned.1.call-update
  15.4 126.4 %all-gather.17.cloned.1.call-done = bf16[1,4096,1024]{2,1,0:T(8,128)(2,1)} async-done(((bf16[1,512,1024]{2,1,0:T(8,128)(2,1)}), bf16[1,4096,1024]{2,1,0:T(8,128)(2,1)}) %all-gather.17.cloned.1.call-update) | async-done | bytes 8388624 | tf_op jit(solution)/shard_map/all_gather | solution.py:51
  141.8 14.0 %gather_fusion.4 = bf16[96,128,1024]{2,1,0:T(8,128)(2,1)} fusion(bf16[32,128,1024]{2,1,0:T(8,128)(2,1)} %bitcast.129, s32[1024]{0:T(1024)S(1)} %pad_clamp_fusion.1), kind=kCustom, calls=%fused_computation.4 | custom fusion | bytes 50332032 | tf_op jit(solution)/shard_map/gather | solution.py:15
  155.8 11.1 %bitcast_convert_fusion.1 = bf16[4,128,1024]{2,1,0:T(8,128)(2,1)S(1)} fusion(bf16[4,24,128,1024]{3,2,1,0:T(8,128)(2,1)} %bitcast.138, bf16[2,4,24,128,128]{4,3,2,1,0:T(8,128)(2,1)} %param.10, pred[4,24]{1,0:T(4,128)(4,1)S(1)} %get-tuple-element.29), kind=kOutput, calls=%fused_computation.26 | convolution fusion | flops 3223322624 | bytes 29360224 | tf_op jit(solution)/shard_map/hgfu,hguq->hfq/dot_general | solution.py:18
  166.9 1.3 copy.24
  168.4 98.2 %all-gather.9.cloned.1.call-done = bf16[1,4096,1024]{2,1,0:T(8,128)(2,1)} async-done(((bf16[1,512,1024]{2,1,0:T(8,128)(2,1)}), bf16[1,4096,1024]{2,1,0:T(8,128)(2,1)}) %all-gather.9.cloned.1.call-update) | async-done | bytes 8388624 | tf_op jit(solution)/shard_map/all_gather | solution.py:51
  266.6 14.3 %gather_fusion = bf16[96,128,1024]{2,1,0:T(8,128)(2,1)} fusion(bf16[32,128,1024]{2,1,0:T(8,128)(2,1)} %bitcast.128, s32[1024]{0:T(1024)S(1)} %pad_clamp_fusion.3), kind=kCustom, calls=%fused_computation | custom fusion | bytes 50332032 | tf_op jit(solution)/shard_map/gather | solution.py:15
  280.9 11.2 %bitcast_convert_fusion.3 = bf16[4,128,1024]{2,1,0:T(8,128)(2,1)S(1)} fusion(bf16[4,24,128,1024]{3,2,1,0:T(8,128)(2,1)} %bitcast.136, bf16[2,4,24,128,128]{4,3,2,1,0:T(8,128)(2,1)} %param.10, pred[4,24]{1,0:T(4,128)(4,1)S(1)} %get-tuple-element.30), kind=kOutput, calls=%fused_computation.28 | convolution fusion | flops 3223322624 | bytes 29360224 | tf_op jit(solution)/shard_map/hgfu,hguq->hfq/dot_general | solution.py:18
  292.0 1.3 copy.18
  293.8 0.6 fusion.25
  295.1 5.7 all-gather.19.cloned.1.call-done
  300.8 6.4 copy.25
  307.2 13.7 %gather_fusion.5 = bf16[192,512,128]{2,1,0:T(8,128)(2,1)} fusion(bf16[512,32,128]{2,0,1:T(8,128)(2,1)} %copy.25, s32[1024]{0:T(1024)S(1)} %pad_clamp_fusion), kind=kCustom, calls=%fused_computation.5 | custom fusion | bytes 50332416 | tf_op jit(solution)/shard_map/gather | solution.py:29
  321.0 15.3 %fusion.3 = f32[8,128,512,1]{2,1,3,0:T(8,128)} fusion(bf16[512,8,24,128]{3,0,2,1:T(8,128)(2,1)} %bitcast.139, bf16[2,8,24,128,128]{4,3,2,1,0:T(8,128)(2,1)} %param.13, pred[8,24]{1,0:T(8,128)(4,1)S(1)} %get-tuple-element.31), kind=kOutput, calls=%fused_computation.13 | convolution fusion | flops 3224371200 | bytes 33554624 | tf_op jit(solution)/shard_map/rtsk,tsck->rtc/dot_general | solution.py:32
  336.3 1.9 copy.26
  338.2 6.4 copy.19
  344.7 13.4 %gather_fusion.1 = bf16[192,512,128]{2,1,0:T(8,128)(2,1)} fusion(bf16[512,32,128]{2,0,1:T(8,128)(2,1)} %copy.19, s32[1024]{0:T(1024)S(1)} %pad_clamp_fusion.2), kind=kCustom, calls=%fused_computation.1 | custom fusion | bytes 50332416 | tf_op jit(solution)/shard_map/gather | solution.py:29
  358.0 15.2 %fusion.1 = f32[8,128,512,1]{2,1,3,0:T(8,128)} fusion(bf16[512,8,24,128]{3,0,2,1:T(8,128)(2,1)} %bitcast.137, bf16[2,8,24,128,128]{4,3,2,1,0:T(8,128)(2,1)} %param.13, pred[8,24]{1,0:T(8,128)(4,1)S(1)} %get-tuple-element.32), kind=kOutput, calls=%fused_computation.11 | convolution fusion | flops 3224371200 | bytes 33554624 | tf_op jit(solution)/shard_map/rtsk,tsck->rtc/dot_general | solution.py:32
  373.2 2.9 copy.20
  376.1 2.9 multiply_reduce_fusion.3
  379.0 39.4 %all-reduce.1 = (f32[1]{0:T(128)}, f32[1]{0:T(128)}) all-reduce(f32[1]{0:T(128)} %bitcast.52, f32[1]{0:T(128)} %bitcast.18), channel_id=1, replica_groups=mesh['row'=8,'col'=4] {'row','col'}, use_global_device_ids=true, to_apply=%region_5.6 | all-reduce | flops 2 | bytes 16 | tf_op jit(solution)/shard_map/psum | solution.py:57
  421.1 5.4 add_convert_fusion.1
  427.1 125.0 %all-gather.21.cloned.1.call-done = bf16[1,4096,1024]{2,1,0:T(8,128)(2,1)} async-done(((bf16[1,512,1024]{2,1,0:T(8,128)(2,1)}), bf16[1,4096,1024]{2,1,0:T(8,128)(2,1)}) %all-gather.21.cloned.1.call-update) | async-done | bytes 8388624 | tf_op jit(solution)/shard_map/all_gather | solution.py:51
  552.2 14.1 %gather_fusion.6 = bf16[96,128,1024]{2,1,0:T(8,128)(2,1)} fusion(bf16[32,128,1024]{2,1,0:T(8,128)(2,1)} %bitcast.131, s32[1024]{0:T(1024)S(1)} %pad_clamp_fusion.1), kind=kCustom, calls=%fused_computation.6 | custom fusion | bytes 50332032 | tf_op jit(solution)/shard_map/gather | solution.py:15
  566.3 11.1 %bitcast_convert_fusion = bf16[4,128,1024]{2,1,0:T(8,128)(2,1)S(1)} fusion(bf16[4,24,128,1024]{3,2,1,0:T(8,128)(2,1)} %bitcast.132, bf16[2,4,24,128,128]{4,3,2,1,0:T(8,128)(2,1)} %param.10, pred[4,24]{1,0:T(4,128)(4,1)S(1)} %get-tuple-element.29), kind=kOutput, calls=%fused_computation.25 | convolution fusion | flops 3223322624 | bytes 29360224 | tf_op jit(solution)/shard_map/hgfu,hguq->hfq/dot_general | solution.py:18
  577.4 1.3 copy.27
  579.0 97.8 %all-gather.13.cloned.1.call-done = bf16[1,4096,1024]{2,1,0:T(8,128)(2,1)} async-done(((bf16[1,512,1024]{2,1,0:T(8,128)(2,1)}), bf16[1,4096,1024]{2,1,0:T(8,128)(2,1)}) %all-gather.13.cloned.1.call-update) | async-done | bytes 8388624 | tf_op jit(solution)/shard_map/all_gather | solution.py:51
  676.9 14.3 %gather_fusion.2 = bf16[96,128,1024]{2,1,0:T(8,128)(2,1)} fusion(bf16[32,128,1024]{2,1,0:T(8,128)(2,1)} %bitcast.130, s32[1024]{0:T(1024)S(1)} %pad_clamp_fusion.3), kind=kCustom, calls=%fused_computation.2 | custom fusion | bytes 50332032 | tf_op jit(solution)/shard_map/gather | solution.py:15
  691.1 11.1 %bitcast_convert_fusion.2 = bf16[4,128,1024]{2,1,0:T(8,128)(2,1)S(1)} fusion(bf16[4,24,128,1024]{3,2,1,0:T(8,128)(2,1)} %bitcast.133, bf16[2,4,24,128,128]{4,3,2,1,0:T(8,128)(2,1)} %param.10, pred[4,24]{1,0:T(4,128)(4,1)S(1)} %get-tuple-element.30), kind=kOutput, calls=%fused_computation.27 | convolution fusion | flops 3223322624 | bytes 29360224 | tf_op jit(solution)/shard_map/hgfu,hguq->hfq/dot_general | solution.py:18
  702.2 1.3 copy.21
  703.6 7.5 all-gather.23.cloned.1.call-done
  711.1 6.4 copy.28
  717.5 13.7 %gather_fusion.7 = bf16[192,512,128]{2,1,0:T(8,128)(2,1)} fusion(bf16[512,32,128]{2,0,1:T(8,128)(2,1)} %copy.28, s32[1024]{0:T(1024)S(1)} %pad_clamp_fusion), kind=kCustom, calls=%fused_computation.7 | custom fusion | bytes 50332416 | tf_op jit(solution)/shard_map/gather | solution.py:29
  731.2 15.3 %fusion.2 = f32[8,128,512,1]{2,1,3,0:T(8,128)} fusion(bf16[512,8,24,128]{3,0,2,1:T(8,128)(2,1)} %bitcast.134, bf16[2,8,24,128,128]{4,3,2,1,0:T(8,128)(2,1)} %param.13, pred[8,24]{1,0:T(8,128)(4,1)S(1)} %get-tuple-element.31), kind=kOutput, calls=%fused_computation.12 | convolution fusion | flops 3224371200 | bytes 33554624 | tf_op jit(solution)/shard_map/rtsk,tsck->rtc/dot_general | solution.py:32
  746.5 1.9 copy.29
  748.5 6.4 copy.22
  755.0 13.4 %gather_fusion.3 = bf16[192,512,128]{2,1,0:T(8,128)(2,1)} fusion(bf16[512,32,128]{2,0,1:T(8,128)(2,1)} %copy.22, s32[1024]{0:T(1024)S(1)} %pad_clamp_fusion.2), kind=kCustom, calls=%fused_computation.3 | custom fusion | bytes 50332416 | tf_op jit(solution)/shard_map/gather | solution.py:29
  768.3 15.2 %fusion = f32[8,128,512,1]{2,1,3,0:T(8,128)} fusion(bf16[512,8,24,128]{3,0,2,1:T(8,128)(2,1)} %bitcast.135, bf16[2,8,24,128,128]{4,3,2,1,0:T(8,128)(2,1)} %param.13, pred[8,24]{1,0:T(8,128)(4,1)S(1)} %get-tuple-element.32), kind=kOutput, calls=%fused_computation.10 | convolution fusion | flops 3224371200 | bytes 33554624 | tf_op jit(solution)/shard_map/rtsk,tsck->rtc/dot_general | solution.py:32
  783.5 2.9 copy.23
  786.4 2.9 multiply_reduce_fusion.2
  789.3 39.4 %all-reduce = (f32[1]{0:T(128)}, f32[1]{0:T(128)}) all-reduce(f32[1]{0:T(128)} %bitcast.66, f32[1]{0:T(128)} %bitcast.32), channel_id=1, replica_groups=mesh['row'=8,'col'=4] {'row','col'}, use_global_device_ids=true, to_apply=%region_7.8 | all-reduce | flops 2 | bytes 16 | tf_op jit(solution)/shard_map/psum | solution.py:57
  831.4 4.1 divide_add_fusion.1
  835.4 2.3 pad_maximum_fusion
  (48 shorter events, 2.4 us)
Async XLA Ops:
  6.5 135.2 %all-gather.17.cloned.1.call-start = ((), (), s32[]{:S(2)}) async-start(), calls=%async_computation.4 | async-start | bytes 9437184 | tf_op jit(solution)/shard_map/all_gather | solution.py:51
  10.7 2.0 copy-start
  12.7 2.5 copy-start.2
  12.7 2.6 copy-start.3
  14.4 252.2 %all-gather.9.cloned.1.call-start = ((), (), s32[]{:S(2)}) async-start(), calls=%async_computation | async-start | bytes 9437184 | tf_op jit(solution)/shard_map/all_gather | solution.py:51
  15.2 285.6 %all-gather.19.cloned.1.call-start = ((), (), s32[]{:S(2)}) async-start(), calls=%async_computation.5 | async-start | bytes 5242880 | tf_op jit(solution)/shard_map/all_gather | solution.py:54
  168.3 170.0 %all-gather.11.cloned.1.call-start = ((), (), s32[]{:S(2)}) async-start(), calls=%async_computation.1 | async-start | bytes 5242880 | tf_op jit(solution)/shard_map/all_gather | solution.py:54
  280.8 12.8 %copy-start.1 = (s32[2,8,24]{2,1,0:T(8,128)S(1)}, s32[2,8,24]{2,1,0:T(8,128)}, u32[]{:S(2)}) copy-start(s32[2,8,24]{2,1,0:T(8,128)} %param.14) | copy-start | bytes 4612
  280.9 13.0 %copy-start.5 = (s32[2]{0:T(128)S(1)}, s32[2]{0:T(128)}, u32[]{:S(2)}) copy-start(s32[2]{0:T(128)} %param.17) | copy-start | bytes 28
  280.9 13.0 %copy-start.6 = (s32[2]{0:T(128)S(1)}, s32[2]{0:T(128)}, u32[]{:S(2)}) copy-start(s32[2]{0:T(128)} %param.16) | copy-start | bytes 28
  280.9 13.6 %copy-start.4 = (s32[2,8]{1,0:T(2,128)S(1)}, s32[2,8]{1,0:T(2,128)}, u32[]{:S(2)}) copy-start(s32[2,8]{1,0:T(2,128)} %param.15) | copy-start | bytes 196
  293.4 258.8 %all-gather.21.cloned.1.call-start = ((), (), s32[]{:S(2)}) async-start(), calls=%async_computation.6 | async-start | bytes 9437184 | tf_op jit(solution)/shard_map/all_gather | solution.py:51
  426.5 250.3 %all-gather.13.cloned.1.call-start = ((), (), s32[]{:S(2)}) async-start(), calls=%async_computation.2 | async-start | bytes 9437184 | tf_op jit(solution)/shard_map/all_gather | solution.py:51
  427.1 284.0 %all-gather.23.cloned.1.call-start = ((), (), s32[]{:S(2)}) async-start(), calls=%async_computation.7 | async-start | bytes 5242880 | tf_op jit(solution)/shard_map/all_gather | solution.py:54
  578.7 169.8 %all-gather.15.cloned.1.call-start = ((), (), s32[]{:S(2)}) async-start(), calls=%async_computation.3 | async-start | bytes 5242880 | tf_op jit(solution)/shard_map/all_gather | solution.py:54
Sparse Core Ops, SparseCore 0:
  14.5 127.1 all-gather.16
  143.9 122.6 all-gather.8
  268.1 32.6 all-gather.18
  302.2 34.4 all-gather.10
  426.6 125.5 all-gather.20
  554.2 122.6 all-gather.12
  678.4 32.6 all-gather.22
  712.6 34.4 all-gather.14
where the time goes:
time: 846 us; the launch traced here: 845 us
  waiting for transfers between devices  462 us (55%)
  local copies, waits for them, and re-layouts  156 us (18%)
  matrix products  105 us (12%)
  blocking collectives  78.8 us (9%)
  other arithmetic  22.5 us (3%)
  between operations  19 us (2%)
    all_gather x4, waiting for transfers between devices, advance(): panel = lax.all_gather(resident_panel_block, 'row', axis=1, tiled=True)  447 us
    psum x2, blocking collectives, advance(): square_sum = lax.psum(jnp.sum(image * image, axis=(1, 2)), ('row', 'col'))  78.8 us
    dot_general x4, matrix products, second_local(): jnp.einsum('rtsk,tsck->rtc', selected_entries, masked_entries, preferred_...  61 us
    gather x4, local copies, waits for them, and re-layouts, first_local(): selected_entries = blocks[columns]  56.7 us
    gather x4, local copies, waits for them, and re-layouts, second_local(): selected_entries = blocks[:, columns]  54.2 us
    dot_general x4, matrix products, first_local(): jnp.einsum('hgfu,hguq->hfq', masked_entries, selected_entries, preferred_...  44.4 us
    another operation x4, local copies, waits for them, and re-layouts, second_local(): blocks = gathered.reshape(height, -1, tile_size)  25.8 us
  transfers between devices with their start and end apart: 8, of which 6 were waited for; matrix products, arithmetic and copies ran while one was open for 22% of the time, Pallas kernels for 0%

commit v1 on v0

--- a/solution.py
+++ b/solution.py
@@ -48,7 +48,7 @@
     s_counts,
 ):
     resident_panel_block = current.astype(jnp.bfloat16)
-    panel = lax.all_gather(resident_panel_block, "row", axis=1, tiled=True)
+    panel = jnp.concatenate(lax.all_gather(resident_panel_block, "row"), 1)
     product = jnp.stack([first_local(first_network_tiles[0], f_columns[0], f_counts[0], panel[0])])
     product = product.astype(jnp.bfloat16)
     gathered = lax.all_gather(product, "col", axis=2, tiled=True)

time: 846 us -> 846 us (level)
  no operation moved by 1% of the time
where the time goes in v1:
time: 846 us; the launch traced here: 845 us
  waiting for transfers between devices  462 us (55%)
  local copies, waits for them, and re-layouts  156 us (18%)
  matrix products  105 us (12%)
  blocking collectives  78.8 us (9%)
  other arithmetic  22.5 us (3%)
  between operations  19 us (2%)
    all_gather x4, waiting for transfers between devices, advance(): panel = jnp.concatenate(lax.all_gather(resident_panel_block, 'row'), 1)  447 us
    psum x2, blocking collectives, advance(): square_sum = lax.psum(jnp.sum(image * image, axis=(1, 2)), ('row', 'col'))  78.8 us
    dot_general x4, matrix products, second_local(): jnp.einsum('rtsk,tsck->rtc', selected_entries, masked_entries, preferred_...  61 us
    gather x4, local copies, waits for them, and re-layouts, first_local(): selected_entries = blocks[columns]  56.7 us
    gather x4, local copies, waits for them, and re-layouts, second_local(): selected_entries = blocks[:, columns]  54.2 us
    dot_general x4, matrix products, first_local(): jnp.einsum('hgfu,hguq->hfq', masked_entries, selected_entries, preferred_...  44.4 us
    another operation x4, local copies, waits for them, and re-layouts, second_local(): blocks = gathered.reshape(height, -1, tile_size)  25.8 us
  transfers between devices with their start and end apart: 8, of which 6 were waited for; matrix products, arithmetic and copies ran while one was open for 22% of the time, Pallas kernels for 0%

profile of v1, /device:TPU:0, one launch (start us, length us, event | category | flops | bytes accessed | tf_op | source)
XLA Modules:
  0.0 844.6 jit_solution(2062341585849978496)
XLA Ops:
  6.5 0.7 broadcast_compare_fusion
  7.3 0.7 broadcast_compare_fusion.1
  8.0 2.7 broadcast_select_fusion
  10.7 2.0 copy-done
  12.7 1.7 fusion.24
  14.5 0.7 all-gather.21.cloned.1.call-update
  15.4 126.4 %all-gather.25.cloned.1.call-done = bf16[8,512,1024]{2,1,0:T(8,128)(2,1)} async-done(((bf16[1,512,1024]{2,1,0:T(8,128)(2,1)}), bf16[8,512,1024]{2,1,0:T(8,128)(2,1)}) %all-gather.25.cloned.1.call-update) | async-done | bytes 8388624 | tf_op jit(solution)/shard_map/all_gather | solution.py:51
  141.8 14.0 %gather_fusion.4 = bf16[96,128,1024]{2,1,0:T(8,128)(2,1)} fusion(bf16[32,128,1024]{2,1,0:T(8,128)(2,1)} %bitcast.129, s32[1024]{0:T(1024)S(1)} %pad_clamp_fusion.1), kind=kCustom, calls=%fused_computation.4 | custom fusion | bytes 50332032 | tf_op jit(solution)/shard_map/gather | solution.py:15
  155.8 11.1 %bitcast_convert_fusion.1 = bf16[4,128,1024]{2,1,0:T(8,128)(2,1)S(1)} fusion(bf16[4,24,128,1024]{3,2,1,0:T(8,128)(2,1)} %bitcast.138, bf16[2,4,24,128,128]{4,3,2,1,0:T(8,128)(2,1)} %param.10, pred[4,24]{1,0:T(4,128)(4,1)S(1)} %get-tuple-element.29), kind=kOutput, calls=%fused_computation.26 | convolution fusion | flops 3223322624 | bytes 29360224 | tf_op jit(solution)/shard_map/hgfu,hguq->hfq/dot_general | solution.py:18
  166.9 1.3 copy.36
  168.4 98.2 %all-gather.21.cloned.1.call-done = bf16[8,512,1024]{2,1,0:T(8,128)(2,1)} async-done(((bf16[1,512,1024]{2,1,0:T(8,128)(2,1)}), bf16[8,512,1024]{2,1,0:T(8,128)(2,1)}) %all-gather.21.cloned.1.call-update) | async-done | bytes 8388624 | tf_op jit(solution)/shard_map/all_gather | solution.py:51
  266.6 14.3 %gather_fusion = bf16[96,128,1024]{2,1,0:T(8,128)(2,1)} fusion(bf16[32,128,1024]{2,1,0:T(8,128)(2,1)} %bitcast.128, s32[1024]{0:T(1024)S(1)} %pad_clamp_fusion.3), kind=kCustom, calls=%fused_computation | custom fusion | bytes 50332032 | tf_op jit(solution)/shard_map/gather | solution.py:15
  280.9 11.2 %bitcast_convert_fusion.3 = bf16[4,128,1024]{2,1,0:T(8,128)(2,1)S(1)} fusion(bf16[4,24,128,1024]{3,2,1,0:T(8,128)(2,1)} %bitcast.136, bf16[2,4,24,128,128]{4,3,2,1,0:T(8,128)(2,1)} %param.10, pred[4,24]{1,0:T(4,128)(4,1)S(1)} %get-tuple-element.30), kind=kOutput, calls=%fused_computation.28 | convolution fusion | flops 3223322624 | bytes 29360224 | tf_op jit(solution)/shard_map/hgfu,hguq->hfq/dot_general | solution.py:18
  292.0 1.3 copy.30
  293.8 0.6 fusion.25
  295.1 5.7 all-gather.17.cloned.1.call-done
  300.8 6.4 copy.37
  307.2 13.7 %gather_fusion.5 = bf16[192,512,128]{2,1,0:T(8,128)(2,1)} fusion(bf16[512,32,128]{2,0,1:T(8,128)(2,1)} %copy.37, s32[1024]{0:T(1024)S(1)} %pad_clamp_fusion), kind=kCustom, calls=%fused_computation.5 | custom fusion | bytes 50332416 | tf_op jit(solution)/shard_map/gather | solution.py:29
  321.0 15.3 %fusion.3 = f32[8,128,512,1]{2,1,3,0:T(8,128)} fusion(bf16[512,8,24,128]{3,0,2,1:T(8,128)(2,1)} %bitcast.139, bf16[2,8,24,128,128]{4,3,2,1,0:T(8,128)(2,1)} %param.13, pred[8,24]{1,0:T(8,128)(4,1)S(1)} %get-tuple-element.31), kind=kOutput, calls=%fused_computation.13 | convolution fusion | flops 3224371200 | bytes 33554624 | tf_op jit(solution)/shard_map/rtsk,tsck->rtc/dot_general | solution.py:32
  336.3 1.9 copy.38
  338.2 6.4 copy.31
  344.7 13.4 %gather_fusion.1 = bf16[192,512,128]{2,1,0:T(8,128)(2,1)} fusion(bf16[512,32,128]{2,0,1:T(8,128)(2,1)} %copy.31, s32[1024]{0:T(1024)S(1)} %pad_clamp_fusion.2), kind=kCustom, calls=%fused_computation.1 | custom fusion | bytes 50332416 | tf_op jit(solution)/shard_map/gather | solution.py:29
  358.0 15.2 %fusion.1 = f32[8,128,512,1]{2,1,3,0:T(8,128)} fusion(bf16[512,8,24,128]{3,0,2,1:T(8,128)(2,1)} %bitcast.137, bf16[2,8,24,128,128]{4,3,2,1,0:T(8,128)(2,1)} %param.13, pred[8,24]{1,0:T(8,128)(4,1)S(1)} %get-tuple-element.32), kind=kOutput, calls=%fused_computation.11 | convolution fusion | flops 3224371200 | bytes 33554624 | tf_op jit(solution)/shard_map/rtsk,tsck->rtc/dot_general | solution.py:32
  373.2 2.9 copy.32
  376.1 2.9 multiply_reduce_fusion.3
  379.0 39.4 %all-reduce.1 = (f32[1]{0:T(128)}, f32[1]{0:T(128)}) all-reduce(f32[1]{0:T(128)} %bitcast.52, f32[1]{0:T(128)} %bitcast.18), channel_id=1, replica_groups=mesh['row'=8,'col'=4] {'row','col'}, use_global_device_ids=true, to_apply=%region_5.6 | all-reduce | flops 2 | bytes 16 | tf_op jit(solution)/shard_map/psum | solution.py:57
  421.1 5.4 add_convert_fusion.1
  427.1 125.0 %all-gather.27.cloned.1.call-done = bf16[8,512,1024]{2,1,0:T(8,128)(2,1)} async-done(((bf16[1,512,1024]{2,1,0:T(8,128)(2,1)}), bf16[8,512,1024]{2,1,0:T(8,128)(2,1)}) %all-gather.27.cloned.1.call-update) | async-done | bytes 8388624 | tf_op jit(solution)/shard_map/all_gather | solution.py:51
  552.2 14.1 %gather_fusion.6 = bf16[96,128,1024]{2,1,0:T(8,128)(2,1)} fusion(bf16[32,128,1024]{2,1,0:T(8,128)(2,1)} %bitcast.131, s32[1024]{0:T(1024)S(1)} %pad_clamp_fusion.1), kind=kCustom, calls=%fused_computation.6 | custom fusion | bytes 50332032 | tf_op jit(solution)/shard_map/gather | solution.py:15
  566.3 11.1 %bitcast_convert_fusion = bf16[4,128,1024]{2,1,0:T(8,128)(2,1)S(1)} fusion(bf16[4,24,128,1024]{3,2,1,0:T(8,128)(2,1)} %bitcast.132, bf16[2,4,24,128,128]{4,3,2,1,0:T(8,128)(2,1)} %param.10, pred[4,24]{1,0:T(4,128)(4,1)S(1)} %get-tuple-element.29), kind=kOutput, calls=%fused_computation.25 | convolution fusion | flops 3223322624 | bytes 29360224 | tf_op jit(solution)/shard_map/hgfu,hguq->hfq/dot_general | solution.py:18
  577.4 1.3 copy.39
  579.0 97.8 %all-gather.23.cloned.1.call-done = bf16[8,512,1024]{2,1,0:T(8,128)(2,1)} async-done(((bf16[1,512,1024]{2,1,0:T(8,128)(2,1)}), bf16[8,512,1024]{2,1,0:T(8,128)(2,1)}) %all-gather.23.cloned.1.call-update) | async-done | bytes 8388624 | tf_op jit(solution)/shard_map/all_gather | solution.py:51
  676.9 14.3 %gather_fusion.2 = bf16[96,128,1024]{2,1,0:T(8,128)(2,1)} fusion(bf16[32,128,1024]{2,1,0:T(8,128)(2,1)} %bitcast.130, s32[1024]{0:T(1024)S(1)} %pad_clamp_fusion.3), kind=kCustom, calls=%fused_computation.2 | custom fusion | bytes 50332032 | tf_op jit(solution)/shard_map/gather | solution.py:15
  691.1 11.1 %bitcast_convert_fusion.2 = bf16[4,128,1024]{2,1,0:T(8,128)(2,1)S(1)} fusion(bf16[4,24,128,1024]{3,2,1,0:T(8,128)(2,1)} %bitcast.133, bf16[2,4,24,128,128]{4,3,2,1,0:T(8,128)(2,1)} %param.10, pred[4,24]{1,0:T(4,128)(4,1)S(1)} %get-tuple-element.30), kind=kOutput, calls=%fused_computation.27 | convolution fusion | flops 3223322624 | bytes 29360224 | tf_op jit(solution)/shard_map/hgfu,hguq->hfq/dot_general | solution.py:18
  702.2 1.3 copy.33
  703.6 7.5 all-gather.19.cloned.1.call-done
  711.1 6.4 copy.40
  717.5 13.7 %gather_fusion.7 = bf16[192,512,128]{2,1,0:T(8,128)(2,1)} fusion(bf16[512,32,128]{2,0,1:T(8,128)(2,1)} %copy.40, s32[1024]{0:T(1024)S(1)} %pad_clamp_fusion), kind=kCustom, calls=%fused_computation.7 | custom fusion | bytes 50332416 | tf_op jit(solution)/shard_map/gather | solution.py:29
  731.2 15.3 %fusion.2 = f32[8,128,512,1]{2,1,3,0:T(8,128)} fusion(bf16[512,8,24,128]{3,0,2,1:T(8,128)(2,1)} %bitcast.134, bf16[2,8,24,128,128]{4,3,2,1,0:T(8,128)(2,1)} %param.13, pred[8,24]{1,0:T(8,128)(4,1)S(1)} %get-tuple-element.31), kind=kOutput, calls=%fused_computation.12 | convolution fusion | flops 3224371200 | bytes 33554624 | tf_op jit(solution)/shard_map/rtsk,tsck->rtc/dot_general | solution.py:32
  746.5 1.9 copy.41
  748.5 6.4 copy.34
  755.0 13.4 %gather_fusion.3 = bf16[192,512,128]{2,1,0:T(8,128)(2,1)} fusion(bf16[512,32,128]{2,0,1:T(8,128)(2,1)} %copy.34, s32[1024]{0:T(1024)S(1)} %pad_clamp_fusion.2), kind=kCustom, calls=%fused_computation.3 | custom fusion | bytes 50332416 | tf_op jit(solution)/shard_map/gather | solution.py:29
  768.3 15.2 %fusion = f32[8,128,512,1]{2,1,3,0:T(8,128)} fusion(bf16[512,8,24,128]{3,0,2,1:T(8,128)(2,1)} %bitcast.135, bf16[2,8,24,128,128]{4,3,2,1,0:T(8,128)(2,1)} %param.13, pred[8,24]{1,0:T(8,128)(4,1)S(1)} %get-tuple-element.32), kind=kOutput, calls=%fused_computation.10 | convolution fusion | flops 3224371200 | bytes 33554624 | tf_op jit(solution)/shard_map/rtsk,tsck->rtc/dot_general | solution.py:32
  783.5 2.9 copy.35
  786.4 2.9 multiply_reduce_fusion.2
  789.3 39.4 %all-reduce = (f32[1]{0:T(128)}, f32[1]{0:T(128)}) all-reduce(f32[1]{0:T(128)} %bitcast.66, f32[1]{0:T(128)} %bitcast.32), channel_id=1, replica_groups=mesh['row'=8,'col'=4] {'row','col'}, use_global_device_ids=true, to_apply=%region_7.8 | all-reduce | flops 2 | bytes 16 | tf_op jit(solution)/shard_map/psum | solution.py:57
  831.4 4.1 divide_add_fusion.1
  835.4 2.3 pad_maximum_fusion
  (48 shorter events, 2.4 us)
Async XLA Ops:
  6.5 135.2 %all-gather.25.cloned.1.call-start = ((), (), s32[]{:S(2)}) async-start(), calls=%async_computation.6 | async-start | bytes 9437184 | tf_op jit(solution)/shard_map/all_gather | solution.py:51
  10.7 2.0 copy-start
  12.7 2.5 copy-start.2
  12.7 2.6 copy-start.3
  14.4 252.2 %all-gather.21.cloned.1.call-start = ((), (), s32[]{:S(2)}) async-start(), calls=%async_computation.4 | async-start | bytes 9437184 | tf_op jit(solution)/shard_map/all_gather | solution.py:51
  15.2 285.6 %all-gather.17.cloned.1.call-start = ((), (), s32[]{:S(2)}) async-start(), calls=%async_computation.2 | async-start | bytes 5242880 | tf_op jit(solution)/shard_map/all_gather | solution.py:54
  168.3 170.0 %all-gather.13.cloned.1.call-start = ((), (), s32[]{:S(2)}) async-start(), calls=%async_computation | async-start | bytes 5242880 | tf_op jit(solution)/shard_map/all_gather | solution.py:54
  280.8 12.8 %copy-start.1 = (s32[2,8,24]{2,1,0:T(8,128)S(1)}, s32[2,8,24]{2,1,0:T(8,128)}, u32[]{:S(2)}) copy-start(s32[2,8,24]{2,1,0:T(8,128)} %param.14) | copy-start | bytes 4612
  280.9 13.0 %copy-start.5 = (s32[2]{0:T(128)S(1)}, s32[2]{0:T(128)}, u32[]{:S(2)}) copy-start(s32[2]{0:T(128)} %param.17) | copy-start | bytes 28
  280.9 13.0 %copy-start.6 = (s32[2]{0:T(128)S(1)}, s32[2]{0:T(128)}, u32[]{:S(2)}) copy-start(s32[2]{0:T(128)} %param.16) | copy-start | bytes 28
  280.9 13.6 %copy-start.4 = (s32[2,8]{1,0:T(2,128)S(1)}, s32[2,8]{1,0:T(2,128)}, u32[]{:S(2)}) copy-start(s32[2,8]{1,0:T(2,128)} %param.15) | copy-start | bytes 196
  293.4 258.8 %all-gather.27.cloned.1.call-start = ((), (), s32[]{:S(2)}) async-start(), calls=%async_computation.7 | async-start | bytes 9437184 | tf_op jit(solution)/shard_map/all_gather | solution.py:51
  426.5 250.3 %all-gather.23.cloned.1.call-start = ((), (), s32[]{:S(2)}) async-start(), calls=%async_computation.5 | async-start | bytes 9437184 | tf_op jit(solution)/shard_map/all_gather | solution.py:51
  427.1 284.0 %all-gather.19.cloned.1.call-start = ((), (), s32[]{:S(2)}) async-start(), calls=%async_computation.3 | async-start | bytes 5242880 | tf_op jit(solution)/shard_map/all_gather | solution.py:54
  578.7 169.8 %all-gather.15.cloned.1.call-start = ((), (), s32[]{:S(2)}) async-start(), calls=%async_computation.1 | async-start | bytes 5242880 | tf_op jit(solution)/shard_map/all_gather | solution.py:54
Sparse Core Ops, SparseCore 0:
  14.5 127.1 all-gather.24
  143.9 122.6 all-gather.20
  268.1 32.6 all-gather.16
  302.2 34.4 all-gather.12
  426.6 125.5 all-gather.26
  554.2 122.6 all-gather.22
  678.4 32.6 all-gather.18
  712.6 34.4 all-gather.14
